TPU v7x, 32 devices: a whole 2x2x4 slice. The times are simulated.
32 devices in a mesh: scen: 8 (over y, x, core), col: 4 (over z).
Axes of the slice: x: 2, y: 2, z: 4, core: 2. Of those that a mesh axis runs over, the one named last changes fastest.
Arguments:
- tech: bfloat16 [32, 2048, 4096], P('scen', None, 'col'), may hold values from -0.046875 to 0.046875
- recourse: bfloat16 [32, 2048, 1024], P('scen', None, 'col'), may hold values from -0.125 to 0.125
- rhs: float32 [32, 32, 2048], P(None, 'scen'), may hold values from -6 to 6
- cost_first: float32 [4096], P('col'), may hold values from -6 to 6
- cost_second: float32 [32, 1024], P('scen', 'col'), may hold values from -6 to 6
- cone_id: int32 [32, 2048], P('scen'), may hold values from 0 to 127, never falling along the last dimension, each value on 1 to 64 neighbouring positions
Outputs:
- first_section: float32 [32, 4096], P(None, 'col')
- second_section: float32 [32, 32, 1024], P(None, 'scen', 'col')
- slack: float32 [32, 32, 2048], P(None, 'scen', 'col')
- dual: float32 [32, 32, 2048], P(None, 'scen', 'col')
Inputs may be any that keep to these rules, and one draw needn't show every extreme that they name: Along the rows of a scenario cone_id never falls; a cone holds 1 to 64 rows.
All inputs are finite; a program needn't handle non-finite values.
Results may differ from a plain program's by a relative error of at most 0.014.
Values may be sent and summed in bfloat16 or wider, within the bound.
A program may use at most 128 MiB of HBM per device.

v0:
```python
import functools

import jax
import jax.numpy as jnp
from jax import lax
from jax.experimental import pallas as pl
from jax.experimental.pallas import tpu as pltpu
from jax.sharding import PartitionSpec as P

NCONE = 128
ITERS = 3
CG_STEPS = 3


HIGH = lax.Precision.HIGHEST


def cone_factors(lead, tail):
    norm_tail = jnp.sqrt(tail)
    inside = norm_tail <= lead
    polar = norm_tail <= -lead
    safe = jnp.where(norm_tail > 0.0, norm_tail, 1.0)
    middle = 0.5 * (lead + norm_tail)
    head = jnp.where(inside, lead, jnp.where(polar, 0.0, middle))
    scale = jnp.where(inside, 1.0, jnp.where(polar, 0.0, middle / safe))
    return (head, scale)


def body(tech, recourse, rhs, cost_first, cost_second, cone_id):
    f32 = jnp.float32
    bf16 = jnp.bfloat16
    n_scen = lax.axis_size("scen")
    n_col = lax.axis_size("col")
    batch = rhs.shape[0]
    scen_local = tech.shape[0]
    rows = tech.shape[1]
    first_cols = tech.shape[2]
    tech_flat = tech.reshape(scen_local * rows, first_cols)
    starts = jnp.concatenate(
        [jnp.ones((scen_local, 1), f32), (cone_id[:, 1:] != cone_id[:, :-1]).astype(f32)], axis=1
    )
    labels = lax.broadcasted_iota(jnp.int32, (1, 1, NCONE), 2)
    onehot = (cone_id[:, :, None] == labels).astype(f32)
    part_rows = rows // n_col
    row_start = lax.axis_index("col") * part_rows
    row_weight = 1.0 / n_col
    share_cols = first_cols // n_scen
    cost_here = lax.dynamic_slice_in_dim(
        cost_first, lax.axis_index("scen") * share_cols, share_cols, 0
    )
    first_weight = 1.0
    start_rows = starts[None]

    def couple(partial_value):
        return lax.psum_scatter(partial_value, "scen", scatter_dimension=1, tiled=True)

    def adjoint(rows_bf):
        first_part = jnp.dot(
            rows_bf.reshape(batch, scen_local * rows), tech_flat, preferred_element_type=f32
        )
        second_part = jnp.einsum("bsm,smk->bsk", rows_bf, recourse, preferred_element_type=f32)
        return (first_part, second_part)

    def local_squares(first_vec, second_vec):
        return first_weight * jnp.sum(first_vec * first_vec, axis=1) + jnp.sum(
            second_vec * second_vec, axis=(1, 2)
        )

    def total_norm(first_vec, second_vec):
        return lax.psum(local_squares(first_vec, second_vec), ("scen", "col"))

    here_rows = rhs.shape[2]
    first_sol = jnp.zeros((batch, share_cols), f32)
    second_sol = jnp.zeros((batch, scen_local, recourse.shape[2]), f32)
    slack = jnp.zeros((batch, scen_local, here_rows), f32)
    dual = jnp.zeros((batch, scen_local, here_rows), f32)
    image = jnp.zeros((batch, scen_local, here_rows), f32)
    for outer in range(ITERS):
        resid_rows = (rhs - slack - dual - image).astype(bf16)
        back_first, back_second = adjoint(resid_rows)
        res_first = couple(back_first) - cost_here[None, :]
        res_second = back_second - cost_second[None]
        res_norm = total_norm(res_first, res_second)
        dir_first, dir_second = (res_first, res_second)
        for step in range(CG_STEPS):
            dir_first_bf = lax.all_gather(dir_first.astype(bf16), "scen", axis=1, tiled=True)
            forward_partial_value = lax.dot_general(
                dir_first_bf, tech_flat, (((1,), (1,)), ((), ())), preferred_element_type=f32
            )
            forward_partial_value = forward_partial_value.reshape(batch, scen_local, rows)
            image_step = lax.psum(
                forward_partial_value
                + jnp.einsum(
                    "bsk,smk->bsm", dir_second.astype(bf16), recourse, preferred_element_type=f32
                ),
                "col",
            )
            curv_term = local_squares(dir_first, dir_second) + row_weight * jnp.sum(
                image_step * image_step, axis=(1, 2)
            )
            curv = lax.psum(curv_term, ("scen", "col"))
            alpha = res_norm / curv
            first_sol = first_sol + alpha[:, None] * dir_first
            second_sol = second_sol + alpha[:, None, None] * dir_second
            image = image + alpha[:, None, None] * image_step
            if step + 1 < CG_STEPS:
                back_first, back_second = adjoint(image_step.astype(bf16))
                res_first = res_first - alpha[:, None] * (dir_first + couple(back_first))
                res_second = res_second - alpha[:, None, None] * (dir_second + back_second)
                new_norm = total_norm(res_first, res_second)
                ratio = new_norm / res_norm
                dir_first = res_first + ratio[:, None] * dir_first
                dir_second = res_second + ratio[:, None, None] * dir_second
                res_norm = new_norm
        values = rhs - image - dual
        project_lead = jnp.einsum("bsm,smc->bsc", values * start_rows, onehot, precision=HIGH)
        project_tail = jnp.einsum(
            "bsm,smc->bsc", values * values * (1.0 - start_rows), onehot, precision=HIGH
        )
        project_lead, project_tail = (project_lead, project_tail)
        head, scale = cone_factors(project_lead, project_tail)
        head_rows = jnp.einsum("bsc,smc->bsm", head, onehot, precision=HIGH)
        scale_rows = jnp.einsum("bsc,smc->bsm", scale, onehot, precision=HIGH)
        slack = start_rows * head_rows + (1.0 - start_rows) * values * scale_rows
        dual = dual + image + slack - rhs
    first_out = lax.all_gather(first_sol, "scen", axis=1, tiled=True)
    slack_out = lax.dynamic_slice_in_dim(slack, row_start, part_rows, 2)
    dual_out = lax.dynamic_slice_in_dim(dual, row_start, part_rows, 2)
    return (first_out, second_sol, slack_out, dual_out)


def kernel_body(
    dims,
    tech_hbm, rec_hbm, rhs_hbm, cost1, cost2, cid, starts,
    x_out, y_out, slack_out, dual_out,
    tech, rec, g, dual, slack, onehot, q_all, part, rsc, q_own,
    acc, snd, rs1, ag1, back2, res2, dir2, res1, dir1,
    nrm_own, nrm1, nrm_mid, nrm2, crv_own, crv1, crv_mid, crv2,
    nres, ratio, alpha, qq, xs,
    ld_t, ld_r, ld_g,
    ag1_s, ag1_r, n1_s, n1_r, n2_s, n2_r, rsc_s, rsc_r, agc_s, agc_r,
    c1_s, c1_r, c2_s, c2_r, rs1_s, rs1_r, fin_s, fin_r,
):
    n_scen, n_col, B, S, R, C1, C2 = dims
    f32, bf16 = jnp.float32, jnp.bfloat16
    RQ = R // n_col
    SH = C1 // n_scen
    G = B // 8
    W = 128 // G
    ms = lax.axis_index("scen")
    mc = lax.axis_index("col")

    def scen_peer(j):
        return lax.rem(ms + j, n_scen)

    def col_peer(j):
        return lax.rem(mc + j, n_col)

    def to_scen(src, dst, ss, rs, j):
        return pltpu.make_async_remote_copy(
            src_ref=src, dst_ref=dst, send_sem=ss, recv_sem=rs,
            device_id=(scen_peer(j), mc), device_id_type=pl.DeviceIdType.MESH)

    def to_col(src, dst, ss, rs, j):
        return pltpu.make_async_remote_copy(
            src_ref=src, dst_ref=dst, send_sem=ss, recv_sem=rs,
            device_id=(ms, col_peer(j)), device_id_type=pl.DeviceIdType.MESH)

    SJ = range(1, n_scen)
    CJ = range(1, n_col)

    def d_ag1(j):
        return to_scen(ag1.at[ms], ag1.at[ms], ag1_s.at[j - 1], ag1_r.at[j - 1], j)

    def d_n1(j):
        return to_scen(nrm_own, nrm1.at[j - 1], n1_s.at[j - 1], n1_r.at[j - 1], j)

    def d_n2(j):
        return to_col(nrm_mid, nrm2.at[j - 1], n2_s.at[j - 1], n2_r.at[j - 1], j)

    def d_rsc(j, s):
        return to_col(part.at[s, col_peer(j)], rsc.at[j - 1, s], rsc_s.at[j - 1, s], rsc_r.at[j - 1, s], j)

    def d_agc(j, s):
        return to_col(q_all.at[s, mc], q_all.at[s, mc], agc_s.at[j - 1, s], agc_r.at[j - 1, s], j)

    def d_c1(j):
        return to_col(crv_own, crv1.at[j - 1], c1_s.at[j - 1], c1_r.at[j - 1], j)

    def d_c2(j):
        return to_scen(crv_mid, crv2.at[j - 1], c2_s.at[j - 1], c2_r.at[j - 1], j)

    def d_rs1(j):
        return to_scen(snd.at[scen_peer(j)], rs1.at[j - 1], rs1_s.at[j - 1], rs1_r.at[j - 1], j)

    def d_fin(j):
        return to_scen(xs.at[ms], xs.at[ms], fin_s.at[j - 1], fin_r.at[j - 1], j)

    group = lax.broadcasted_iota(jnp.int32, (8, 128), 1) // W

    def pack(x):
        shift = 64
        while shift >= W:
            x = x + pltpu.roll(x, shift, 1)
            shift //= 2
        out = x[0:8]
        for k in range(1, G):
            out = jnp.where(group == k, x[8 * k:8 * k + 8], out)
        return out

    def unpack(p):
        return jnp.concatenate(
            [jnp.broadcast_to(jnp.sum(jnp.where(group == k, p, 0.0), axis=1, keepdims=True), (8, 128))
             for k in range(G)], axis=0)

    def lanes(x):
        out = x[:, 0:128]
        for k in range(1, x.shape[1] // 128):
            out = out + x[:, 128 * k:128 * k + 128]
        return out

    def load_t(s):
        return pltpu.make_async_copy(tech_hbm.at[s], tech.at[s], ld_t.at[s])

    def load_r(s):
        return pltpu.make_async_copy(rec_hbm.at[s], rec.at[s], ld_r.at[s])

    load_g = pltpu.make_async_copy(rhs_hbm, g, ld_g)
    load_g.start()
    for s in range(S):
        load_t(s).start()
        load_r(s).start()

    barrier = pltpu.get_barrier_semaphore()
    for j in SJ:
        pl.semaphore_signal(barrier, inc=1, device_id=(scen_peer(j), mc), device_id_type=pl.DeviceIdType.MESH)
    for j in CJ:
        pl.semaphore_signal(barrier, inc=1, device_id=(ms, col_peer(j)), device_id_type=pl.DeviceIdType.MESH)

    dir1[...] = jnp.zeros_like(dir1)
    dir2[...] = jnp.zeros_like(dir2)
    q_own[...] = jnp.zeros_like(q_own)
    dual[...] = jnp.zeros_like(dual)
    xs[ms] = jnp.zeros((B, SH), f32)
    y_out[...] = jnp.zeros_like(y_out)
    load_g.wait()

    def init(s, c):
        ids = cid[pl.ds(s, 1), :]
        onehot[s] = (lax.broadcasted_iota(jnp.int32, (NCONE, R), 0) == ids).astype(f32).astype(bf16)
        for k in range(n_col):
            q_all[s, k] = g[s, :, k * RQ:(k + 1) * RQ].astype(bf16)
        return c

    lax.fori_loop(0, S, init, 0)
    pl.semaphore_wait(barrier, n_scen + n_col - 2)

    def curv_forward():
        total = crv_own[...]
        for j in CJ:
            d_c1(j).wait_recv()
            total = total + crv1[j - 1]
        for j in CJ:
            d_c1(j).wait_send()
        crv_mid[...] = total
        for j in SJ:
            d_c2(j).start()

    def curv_finish():
        total = crv_mid[...]
        for j in SJ:
            d_c2(j).wait_recv()
            total = total + crv2[j - 1]
        for j in SJ:
            d_c2(j).wait_send()
        alpha[...] = nres[...] / unpack(total)

    def advance():
        a = alpha[...][:, 0:1]
        xs[ms] = xs[ms] + a * dir1[...]

        def one(s, c):
            y_out[s] = y_out[s] + a * dir2[s]
            for k in range(n_col):
                cols = slice(k * RQ, (k + 1) * RQ)
                g[s, :, cols] = g[s, :, cols] - a * q_all[s, k].astype(f32)
            return c

        lax.fori_loop(0, S, one, 0)

    def split(x):
        hi = x.astype(bf16)
        return [hi, (x - hi.astype(f32)).astype(bf16)]

    def project(s, c):
        st = starts[pl.ds(s, 1), :]
        v = g[s] - dual[s]
        lead_v = v * st
        tail_v = v * v * (1.0 - st)
        stack = jnp.concatenate(split(lead_v) + split(tail_v), axis=0)
        sums = lax.dot_general(stack, onehot[s], (((1,), (1,)), ((), ())), preferred_element_type=f32)
        lead = sums[0:B] + sums[B:2 * B]
        tail = sums[2 * B:3 * B] + sums[3 * B:4 * B]
        head, scale = cone_factors(lead, tail)
        stack2 = jnp.concatenate(split(head) + split(scale), axis=0)
        outs = jnp.dot(stack2, onehot[s], preferred_element_type=f32)
        head_rows = outs[0:B] + outs[B:2 * B]
        scale_rows = outs[2 * B:3 * B] + outs[3 * B:4 * B]
        sl = st * head_rows + (1.0 - st) * v * scale_rows
        du = sl - v
        slack[s] = sl
        dual[s] = du
        d = g[s] - sl - du
        for k in range(n_col):
            q_all[s, k] = d[:, k * RQ:(k + 1) * RQ].astype(bf16)
        return c

    def step_body(t, carry):
        step = lax.rem(t, CG_STEPS)
        acc[...] = jnp.zeros_like(acc)

        def back(s, c):
            @pl.when(t == 0)
            def _():
                load_t(s).wait()
                load_r(s).wait()

            @pl.when(step != 0)
            def _():
                for j in CJ:
                    d_agc(j, s).wait_recv()
                for j in CJ:
                    d_agc(j, s).wait_send()

            z = jnp.concatenate([q_all[s, k] for k in range(n_col)], axis=1)
            f = jnp.dot(z, tech[s], preferred_element_type=f32)
            for i in range(n_scen):
                acc[i] = acc[i] + f[:, i * SH:(i + 1) * SH]
            back2[s] = jnp.dot(z, rec[s], preferred_element_type=f32)

            @pl.when(jnp.logical_and(step != 0, s == S - 1))
            def _():
                curv_forward()

            return c

        lax.fori_loop(0, S, back, 0)
        for i in range(n_scen):
            snd[i] = acc[i].astype(bf16)
        for j in SJ:
            d_rs1(j).start()

        @pl.when(step != 0)
        def _():
            curv_finish()

        tot = acc[ms]
        for j in SJ:
            d_rs1(j).wait_recv()
            tot = tot + rs1[j - 1].astype(f32)
        for j in SJ:
            d_rs1(j).wait_send()

        @pl.when(step == 0)
        def _():
            res1[...] = tot - cost1[:, pl.ds(pl.multiple_of(ms * SH, 128), SH)]
            for s in range(S):
                res2[s] = back2[s] - cost2[s:s + 1, :]

        @pl.when(step != 0)
        def _():
            a = alpha[...][:, 0:1]
            res1[...] = res1[...] - a * (dir1[...] + tot)
            for s in range(S):
                res2[s] = res2[s] - a * (dir2[s] + back2[s])

        r1 = res1[...]
        ag1[ms] = r1.astype(bf16)
        for j in SJ:
            d_ag1(j).start()
        sq = lanes(r1 * r1)
        for s in range(S):
            r2 = res2[s]
            sq = sq + lanes(r2 * r2)
        nrm_own[...] = pack(sq)
        for j in SJ:
            d_n1(j).start()

        @pl.when(step != 0)
        def _():
            advance()

        for j in SJ:
            d_ag1(j).wait_recv()
        for j in SJ:
            d_ag1(j).wait_send()

        def norm_forward():
            total = nrm_own[...]
            for j in SJ:
                d_n1(j).wait_recv()
                total = total + nrm1[j - 1]
            for j in SJ:
                d_n1(j).wait_send()
            nrm_mid[...] = total
            for j in CJ:
                d_n2(j).start()

        def norm_finish():
            total = nrm_mid[...]
            for j in CJ:
                d_n2(j).wait_recv()
                total = total + nrm2[j - 1]
            for j in CJ:
                d_n2(j).wait_send()
            new = unpack(total)

            @pl.when(step == 0)
            def _():
                ratio[...] = jnp.zeros_like(ratio)

            @pl.when(step != 0)
            def _():
                ratio[...] = new / nres[...]

            nres[...] = new
            r = ratio[...][:, 0:1]
            d1 = res1[...] + r * dir1[...]
            dir1[...] = d1
            dsq = lanes(d1 * d1)
            for s in range(S):
                d2 = res2[s] + r * dir2[s]
                dir2[s] = d2
                dsq = dsq + lanes(d2 * d2)
            qq[...] = dsq

        def process(s):
            r = ratio[...][:, 0:1]
            q = part[s, mc].astype(f32)
            for j in CJ:
                d_rsc(j, s).wait_recv()
                q = q + rsc[j - 1, s].astype(f32)
            q = q + r * q_own[s]
            q_own[s] = q
            q_all[s, mc] = q.astype(bf16)
            for j in CJ:
                d_agc(j, s).start()
            qq[...] = qq[...] + lanes(q * q)

        def front(s, c):
            x = jnp.concatenate([ag1[i] for i in range(n_scen)], axis=1)
            y = res2[s].astype(bf16)
            dn = (((1,), (1,)), ((), ()))
            for k in range(n_col):
                rows = pl.ds(k * RQ, RQ)
                p = lax.dot_general(x, tech[s, rows, :], dn, preferred_element_type=f32)
                p = p + lax.dot_general(y, rec[s, rows, :], dn, preferred_element_type=f32)
                part[s, k] = p.astype(bf16)

            @pl.when(s == 0)
            def _():
                norm_forward()

            for j in CJ:
                d_rsc(j, s).start()
            return c

        lax.fori_loop(0, S, front, 0)
        norm_finish()

        def drain(s, c):
            process(s)
            return c

        lax.fori_loop(0, S, drain, 0)
        crv_own[...] = pack(qq[...])
        for j in CJ:
            d_c1(j).start()
        for s in range(S):
            for j in CJ:
                d_rsc(j, s).wait_send()

        @pl.when(step == CG_STEPS - 1)
        def _():
            curv_forward()

            def arrive(s, c):
                for j in CJ:
                    d_agc(j, s).wait_recv()
                for j in CJ:
                    d_agc(j, s).wait_send()
                return c

            lax.fori_loop(0, S, arrive, 0)
            curv_finish()
            advance()
            lax.fori_loop(0, S, project, 0)

        return carry

    lax.fori_loop(0, ITERS * CG_STEPS, step_body, 0)

    for j in SJ:
        d_fin(j).start()
    here = pl.ds(pl.multiple_of(mc * RQ, 128), RQ)
    for s in range(S):
        slack_out[s] = slack[s, :, here]
        dual_out[s] = dual[s, :, here]
    for j in SJ:
        d_fin(j).wait_recv()
    for j in SJ:
        d_fin(j).wait_send()
    for i in range(n_scen):
        x_out[:, i * SH:(i + 1) * SH] = xs[i]


def fused(tech, recourse, rhs, cost_first, cost_second, cone_id):
    f32, bf16 = jnp.float32, jnp.bfloat16
    n_scen = lax.axis_size("scen")
    n_col = lax.axis_size("col")
    B = rhs.shape[0]
    S, R, C1 = tech.shape
    C2 = recourse.shape[2]
    RQ = R // n_col
    SH = C1 // n_scen
    starts = jnp.concatenate(
        [jnp.ones((S, 1), f32), (cone_id[:, 1:] != cone_id[:, :-1]).astype(f32)], axis=1)
    vm = pl.BlockSpec(memory_space=pltpu.VMEM)
    hbm = pl.BlockSpec(memory_space=pl.ANY)
    V = pltpu.VMEM
    D = pltpu.SemaphoreType.DMA
    ns, nc = n_scen - 1, n_col - 1
    scratch = [
        V((S, R, C1), bf16), V((S, R, C2), bf16),
        V((S, B, R), f32), V((S, B, R), f32), V((S, B, R), f32),
        V((S, NCONE, R), bf16),
        V((S, n_col, B, RQ), bf16), V((S, n_col, B, RQ), bf16), V((nc, S, B, RQ), bf16),
        V((S, B, RQ), f32),
        V((n_scen, B, SH), f32), V((n_scen, B, SH), bf16), V((ns, B, SH), bf16), V((n_scen, B, SH), bf16),
        V((S, B, C2), f32), V((S, B, C2), f32), V((S, B, C2), f32),
        V((B, SH), f32), V((B, SH), f32),
        V((8, 128), f32), V((ns, 8, 128), f32), V((8, 128), f32), V((nc, 8, 128), f32),
        V((8, 128), f32), V((nc, 8, 128), f32), V((8, 128), f32), V((ns, 8, 128), f32),
        V((B, 128), f32), V((B, 128), f32), V((B, 128), f32), V((B, 128), f32),
        V((n_scen, B, SH), f32),
        D((S,)), D((S,)), D,
        D((ns,)), D((ns,)), D((ns,)), D((ns,)), D((nc,)), D((nc,)),
        D((nc, S)), D((nc, S)), D((nc, S)), D((nc, S)),
        D((nc,)), D((nc,)), D((ns,)), D((ns,)), D((ns,)), D((ns,)), D((ns,)), D((ns,)),
    ]
    x, y, slack, dual = pl.pallas_call(
        functools.partial(kernel_body, (n_scen, n_col, B, S, R, C1, C2)),
        out_shape=(
            jax.ShapeDtypeStruct((B, C1), f32),
            jax.ShapeDtypeStruct((S, B, C2), f32),
            jax.ShapeDtypeStruct((S, B, RQ), f32),
            jax.ShapeDtypeStruct((S, B, RQ), f32),
        ),
        in_specs=[hbm, hbm, hbm, vm, vm, vm, vm],
        out_specs=(vm, vm, vm, vm),
        scratch_shapes=scratch,
        compiler_params=pltpu.CompilerParams(
            collective_id=0, has_side_effects=True, vmem_limit_bytes=58 * 1024 * 1024),
    )(
        tech, recourse, jnp.transpose(rhs, (1, 0, 2)),
        cost_first.reshape(1, C1), cost_second, cone_id, starts,
    )
    back = lambda a: jnp.transpose(a, (1, 0, 2))
    return x, back(y), back(slack), back(dual)


def program(tech, recourse, rhs, cost_first, cost_second, cone_id):
    n_scen = lax.axis_size("scen")
    n_col = lax.axis_size("col")
    batch = rhs.shape[0]
    fits = (
        tech.shape[2] % (128 * n_scen) == 0
        and tech.shape[1] % (128 * n_col) == 0
        and recourse.shape[2] % 128 == 0
        and batch % 16 == 0
        and 1024 % batch == 0
        and n_scen > 1
        and n_col > 1
    )
    run = fused if fits else body
    return run(tech, recourse, rhs, cost_first, cost_second, cone_id)


def solution(mesh):
    placed = (
        P("scen", None, "col"),
        P("scen", None, "col"),
        P(None, "scen", None),
        P("col"),
        P("scen", "col"),
        P("scen", None),
    )
    return jax.shard_map(
        program,
        mesh=mesh,
        in_specs=placed,
        out_specs=(
            P(None, "col"),
            P(None, "scen", "col"),
            P(None, "scen", "col"),
            P(None, "scen", "col"),
        ),
        check_vma=False,
    )
```

profile of v0, /device:TPU:0, one launch (start us, length us, event | category | flops | bytes accessed | tf_op | source)
XLA Modules:
  0.0 365.5 jit_solution(17703194291456219605)
XLA Ops:
  0.6 0.9 slice_compare_fusion
  1.6 0.7 pad_convert_fusion.starts
  2.3 2.8 copy.15
  5.1 353.6 %shard_map.93 = (f32[32,1024]{1,0:T(8,128)}, f32[4,32,256]{2,1,0:T(8,128)}, f32[4,32,512]{2,1,0:T(8,128)}, f32[4,32,512]{2,1,0:T(8,128)}) custom-call(bf16[4,2048,1024]{2,1,0:T(8,128)(2,1)} %tech_hbm.1, bf16[4,2048,256]{2,1,0:T(8,128)(2,1)} %rec_hbm.1, f32[4,32,2048]{2,1,0:T(8,128)} %bitcast.7, f32[1,1024]{1,0:T(1,128)} %bitcast.11, f32[4,256]{1,0:T(4,128)} %cost2.1, ...), custom_call_target="tpu_custom_call" | custom-call | tf_op jit(solution)/shard_map/pallas_call | solution.py:551
  358.7 1.6 copy.11
  360.3 1.8 copy.12
  362.1 1.8 copy.13
  364.0 1.6 copy.17
where the time goes:
time: 366 us
  Pallas kernels  354 us (97%)
  local copies, waits for them, and re-layouts  9.68 us (3%)
    pallas_call x1, Pallas kernels, fused(): pl.pallas_call(functools.partial(kernel_body, (n_scen, n_col, B, S, R, C1...  354 us
    unnamed x5, local copies, waits for them, and re-layouts  9.68 us

commit v1 on v0

--- a/solution.py
+++ b/solution.py
@@ -10,6 +10,8 @@
 NCONE = 128
 ITERS = 3
 CG_STEPS = 3
+LAG_A = 4
+LAG_B = 8
 
 
 HIGH = lax.Precision.HIGHEST
@@ -133,22 +135,28 @@
     dims,
     tech_hbm, rec_hbm, rhs_hbm, cost1, cost2, cid, starts,
     x_out, y_out, slack_out, dual_out,
-    tech, rec, g, dual, slack, onehot, q_all, part, rsc, q_own,
+    wts, g, dual, slack, onehot, part, pb, rcv_a, rcv_b, q_own, q_all,
     acc, snd, rs1, ag1, back2, res2, dir2, res1, dir1,
     nrm_own, nrm1, nrm_mid, nrm2, crv_own, crv1, crv_mid, crv2,
-    nres, ratio, alpha, qq, xs,
+    nres, ratio, alpha, qq, dq, xs,
     ld_t, ld_r, ld_g,
-    ag1_s, ag1_r, n1_s, n1_r, n2_s, n2_r, rsc_s, rsc_r, agc_s, agc_r,
+    ag1_s, ag1_r, n1_s, n1_r, n2_s, n2_r, a_s, a_r, b_s, b_r, q_s, q_r,
     c1_s, c1_r, c2_s, c2_r, rs1_s, rs1_r, fin_s, fin_r,
 ):
     n_scen, n_col, B, S, R, C1, C2 = dims
     f32, bf16 = jnp.float32, jnp.bfloat16
-    RQ = R // n_col
+    H = n_col
+    RH = R // H
+    N = S * H
     SH = C1 // n_scen
     G = B // 8
     W = 128 // G
     ms = lax.axis_index("scen")
     mc = lax.axis_index("col")
+    pair = mc + 1 - 2 * lax.rem(mc, 2)
+    across = 3 - mc
+    is_end = jnp.logical_or(mc == 0, mc == 3)
+    is_mid = jnp.logical_or(mc == 1, mc == 2)
 
     def scen_peer(j):
         return lax.rem(ms + j, n_scen)
@@ -161,10 +169,10 @@
             src_ref=src, dst_ref=dst, send_sem=ss, recv_sem=rs,
             device_id=(scen_peer(j), mc), device_id_type=pl.DeviceIdType.MESH)
 
-    def to_col(src, dst, ss, rs, j):
+    def to_col(src, dst, ss, rs, target):
         return pltpu.make_async_remote_copy(
             src_ref=src, dst_ref=dst, send_sem=ss, recv_sem=rs,
-            device_id=(ms, col_peer(j)), device_id_type=pl.DeviceIdType.MESH)
+            device_id=(ms, target), device_id_type=pl.DeviceIdType.MESH)
 
     SJ = range(1, n_scen)
     CJ = range(1, n_col)
@@ -176,16 +184,19 @@
         return to_scen(nrm_own, nrm1.at[j - 1], n1_s.at[j - 1], n1_r.at[j - 1], j)
 
     def d_n2(j):
-        return to_col(nrm_mid, nrm2.at[j - 1], n2_s.at[j - 1], n2_r.at[j - 1], j)
-
-    def d_rsc(j, s):
-        return to_col(part.at[s, col_peer(j)], rsc.at[j - 1, s], rsc_s.at[j - 1, s], rsc_r.at[j - 1, s], j)
-
-    def d_agc(j, s):
-        return to_col(q_all.at[s, mc], q_all.at[s, mc], agc_s.at[j - 1, s], agc_r.at[j - 1, s], j)
+        return to_col(nrm_mid, nrm2.at[j - 1], n2_s.at[j - 1], n2_r.at[j - 1], col_peer(j))
+
+    def d_a(c):
+        return to_col(pb.at[c], rcv_a.at[c], a_s.at[c], a_r.at[c], pair)
+
+    def d_b(c):
+        return to_col(pb.at[c], rcv_b.at[c], b_s.at[c], b_r.at[c], across)
+
+    def d_q(c):
+        return to_col(q_all.at[c], q_all.at[c], q_s.at[c], q_r.at[c], pair)
 
     def d_c1(j):
-        return to_col(crv_own, crv1.at[j - 1], c1_s.at[j - 1], c1_r.at[j - 1], j)
+        return to_col(crv_own, crv1.at[j - 1], c1_s.at[j - 1], c1_r.at[j - 1], col_peer(j))
 
     def d_c2(j):
         return to_scen(crv_mid, crv2.at[j - 1], c2_s.at[j - 1], c2_r.at[j - 1], j)
@@ -219,17 +230,34 @@
             out = out + x[:, 128 * k:128 * k + 128]
         return out
 
-    def load_t(s):
-        return pltpu.make_async_copy(tech_hbm.at[s], tech.at[s], ld_t.at[s])
-
-    def load_r(s):
-        return pltpu.make_async_copy(rec_hbm.at[s], rec.at[s], ld_r.at[s])
-
-    load_g = pltpu.make_async_copy(rhs_hbm, g, ld_g)
-    load_g.start()
-    for s in range(S):
-        load_t(s).start()
-        load_r(s).start()
+    def rows_of(c):
+        return c // H, pl.ds(pl.multiple_of(lax.rem(c, H) * RH, RH), RH)
+
+    def load_t(c):
+        s, rows = rows_of(c)
+        return pltpu.make_async_copy(tech_hbm.at[s, rows, :], wts.at[c, :, pl.ds(0, C1)], ld_t.at[c])
+
+    def load_r(c):
+        s, rows = rows_of(c)
+        return pltpu.make_async_copy(rec_hbm.at[s, rows, :], wts.at[c, :, pl.ds(C1, C2)], ld_r.at[c])
+
+    def load_g(c):
+        s, rows = rows_of(c)
+        return pltpu.make_async_copy(rhs_hbm.at[s, :, rows], g.at[c], ld_g.at[c])
+
+    def each(n, f):
+        def one(c, carry):
+            f(c)
+            return carry
+        lax.fori_loop(0, n, one, 0)
+
+    each(N, lambda c: load_g(c).start())
+
+    def load_w(c):
+        load_t(c).start()
+        load_r(c).start()
+
+    each(N, load_w)
 
     barrier = pltpu.get_barrier_semaphore()
     for j in SJ:
@@ -243,16 +271,38 @@
     dual[...] = jnp.zeros_like(dual)
     xs[ms] = jnp.zeros((B, SH), f32)
     y_out[...] = jnp.zeros_like(y_out)
-    load_g.wait()
-
-    def init(s, c):
+
+    def init(c):
+        load_g(c).wait()
+        q_all[c] = g[c].astype(bf16)
+
+    each(N, init)
+
+    def init_cones(s):
         ids = cid[pl.ds(s, 1), :]
         onehot[s] = (lax.broadcasted_iota(jnp.int32, (NCONE, R), 0) == ids).astype(f32).astype(bf16)
-        for k in range(n_col):
-            q_all[s, k] = g[s, :, k * RQ:(k + 1) * RQ].astype(bf16)
-        return c
-
-    lax.fori_loop(0, S, init, 0)
+
+    each(S, init_cones)
+
+    def clear_back():
+        acc[...] = jnp.zeros_like(acc)
+        back2[...] = jnp.zeros_like(back2)
+
+    def back(c):
+        s = c // H
+        f = jnp.dot(q_all[c], wts[c], preferred_element_type=f32)
+        for i in range(n_scen):
+            acc[i] = acc[i] + f[:, i * SH:(i + 1) * SH]
+        back2[s] = back2[s] + f[:, C1:C1 + C2]
+
+    clear_back()
+
+    def first_back(c):
+        load_t(c).wait()
+        load_r(c).wait()
+        back(c)
+
+    each(N, first_back)
     pl.semaphore_wait(barrier, n_scen + n_col - 2)
 
     def curv_forward():
@@ -278,23 +328,22 @@
     def advance():
         a = alpha[...][:, 0:1]
         xs[ms] = xs[ms] + a * dir1[...]
-
-        def one(s, c):
+        for s in range(S):
             y_out[s] = y_out[s] + a * dir2[s]
-            for k in range(n_col):
-                cols = slice(k * RQ, (k + 1) * RQ)
-                g[s, :, cols] = g[s, :, cols] - a * q_all[s, k].astype(f32)
-            return c
-
-        lax.fori_loop(0, S, one, 0)
+
+        def one(c):
+            g[c] = g[c] - a * q_all[c].astype(f32)
+
+        each(N, one)
 
     def split(x):
         hi = x.astype(bf16)
         return [hi, (x - hi.astype(f32)).astype(bf16)]
 
-    def project(s, c):
+    def project(s):
         st = starts[pl.ds(s, 1), :]
-        v = g[s] - dual[s]
+        gs = jnp.concatenate([g[s * H + h] for h in range(H)], axis=1)
+        v = gs - jnp.concatenate([dual[s * H + h] for h in range(H)], axis=1)
         lead_v = v * st
         tail_v = v * v * (1.0 - st)
         stack = jnp.concatenate(split(lead_v) + split(tail_v), axis=0)
@@ -308,43 +357,27 @@
         scale_rows = outs[2 * B:3 * B] + outs[3 * B:4 * B]
         sl = st * head_rows + (1.0 - st) * v * scale_rows
         du = sl - v
-        slack[s] = sl
-        dual[s] = du
-        d = g[s] - sl - du
-        for k in range(n_col):
-            q_all[s, k] = d[:, k * RQ:(k + 1) * RQ].astype(bf16)
-        return c
+        d = (gs - sl - du).astype(bf16)
+        for h in range(H):
+            cols = slice(h * RH, (h + 1) * RH)
+            slack[s * H + h] = sl[:, cols]
+            dual[s * H + h] = du[:, cols]
+            q_all[s * H + h] = d[:, cols]
+
+    def norm_forward():
+        total = nrm_own[...]
+        for j in SJ:
+            d_n1(j).wait_recv()
+            total = total + nrm1[j - 1]
+        for j in SJ:
+            d_n1(j).wait_send()
+        nrm_mid[...] = total
+        for j in CJ:
+            d_n2(j).start()
 
     def step_body(t, carry):
         step = lax.rem(t, CG_STEPS)
-        acc[...] = jnp.zeros_like(acc)
-
-        def back(s, c):
-            @pl.when(t == 0)
-            def _():
-                load_t(s).wait()
-                load_r(s).wait()
-
-            @pl.when(step != 0)
-            def _():
-                for j in CJ:
-                    d_agc(j, s).wait_recv()
-                for j in CJ:
-                    d_agc(j, s).wait_send()
-
-            z = jnp.concatenate([q_all[s, k] for k in range(n_col)], axis=1)
-            f = jnp.dot(z, tech[s], preferred_element_type=f32)
-            for i in range(n_scen):
-                acc[i] = acc[i] + f[:, i * SH:(i + 1) * SH]
-            back2[s] = jnp.dot(z, rec[s], preferred_element_type=f32)
-
-            @pl.when(jnp.logical_and(step != 0, s == S - 1))
-            def _():
-                curv_forward()
-
-            return c
-
-        lax.fori_loop(0, S, back, 0)
+        last = step == CG_STEPS - 1
         for i in range(n_scen):
             snd[i] = acc[i].astype(bf16)
         for j in SJ:
@@ -352,14 +385,13 @@
 
         @pl.when(step != 0)
         def _():
+            curv_forward()
             curv_finish()
 
         tot = acc[ms]
         for j in SJ:
             d_rs1(j).wait_recv()
             tot = tot + rs1[j - 1].astype(f32)
-        for j in SJ:
-            d_rs1(j).wait_send()
 
         @pl.when(step == 0)
         def _():
@@ -385,26 +417,18 @@
         nrm_own[...] = pack(sq)
         for j in SJ:
             d_n1(j).start()
+        for j in SJ:
+            d_rs1(j).wait_send()
 
         @pl.when(step != 0)
         def _():
             advance()
 
+        clear_back()
         for j in SJ:
             d_ag1(j).wait_recv()
         for j in SJ:
             d_ag1(j).wait_send()
-
-        def norm_forward():
-            total = nrm_own[...]
-            for j in SJ:
-                d_n1(j).wait_recv()
-                total = total + nrm1[j - 1]
-            for j in SJ:
-                d_n1(j).wait_send()
-            nrm_mid[...] = total
-            for j in CJ:
-                d_n2(j).start()
 
         def norm_finish():
             total = nrm_mid[...]
@@ -432,69 +456,99 @@
                 d2 = res2[s] + r * dir2[s]
                 dir2[s] = d2
                 dsq = dsq + lanes(d2 * d2)
-            qq[...] = dsq
-
-        def process(s):
-            r = ratio[...][:, 0:1]
-            q = part[s, mc].astype(f32)
+            dq[...] = dsq
+
+        def front(c):
+            x = jnp.concatenate([ag1[i] for i in range(n_scen)] + [res2[c // H].astype(bf16)], axis=1)
+            return lax.dot_general(x, wts[c], (((1,), (1,)), ((), ())), preferred_element_type=f32)
+
+        def send_curv(sq):
+            crv_own[...] = pack(sq)
             for j in CJ:
-                d_rsc(j, s).wait_recv()
-                q = q + rsc[j - 1, s].astype(f32)
-            q = q + r * q_own[s]
-            q_own[s] = q
-            q_all[s, mc] = q.astype(bf16)
-            for j in CJ:
-                d_agc(j, s).start()
-            qq[...] = qq[...] + lanes(q * q)
-
-        def front(s, c):
-            x = jnp.concatenate([ag1[i] for i in range(n_scen)], axis=1)
-            y = res2[s].astype(bf16)
-            dn = (((1,), (1,)), ((), ()))
-            for k in range(n_col):
-                rows = pl.ds(k * RQ, RQ)
-                p = lax.dot_general(x, tech[s, rows, :], dn, preferred_element_type=f32)
-                p = p + lax.dot_general(y, rec[s, rows, :], dn, preferred_element_type=f32)
-                part[s, k] = p.astype(bf16)
-
-            @pl.when(s == 0)
-            def _():
-                norm_forward()
-
-            for j in CJ:
-                d_rsc(j, s).start()
-            return c
-
-        lax.fori_loop(0, S, front, 0)
-        norm_finish()
-
-        def drain(s, c):
-            process(s)
-            return c
-
-        lax.fori_loop(0, S, drain, 0)
-        crv_own[...] = pack(qq[...])
-        for j in CJ:
-            d_c1(j).start()
-        for s in range(S):
-            for j in CJ:
-                d_rsc(j, s).wait_send()
-
-        @pl.when(step == CG_STEPS - 1)
+                d_c1(j).start()
+
+        @pl.when(is_end)
+        def _():
+            def go(c):
+                pb[c] = front(c).astype(bf16)
+                d_a(c).start()
+
+                @pl.when(c == 1)
+                def _():
+                    norm_forward()
+
+            each(N, go)
+            norm_finish()
+            send_curv(dq[...])
+
+            def take(c):
+                d_q(c).wait_recv()
+
+                @pl.when(jnp.logical_not(last))
+                def _():
+                    back(c)
+
+            each(N, take)
+            each(N, lambda c: d_a(c).wait_send())
+
+        @pl.when(is_mid)
+        def _():
+            qq[...] = jnp.zeros_like(qq)
+
+            def go(i):
+                @pl.when(i < N)
+                def _():
+                    part[i] = front(i)
+
+                @pl.when(i == 1)
+                def _():
+                    norm_forward()
+
+                @pl.when(jnp.logical_and(i >= LAG_A, i < N + LAG_A))
+                def _():
+                    c = i - LAG_A
+                    d_a(c).wait_recv()
+                    pb[c] = (part[c] + rcv_a[c].astype(f32)).astype(bf16)
+                    d_b(c).start()
+
+                @pl.when(i == LAG_B)
+                def _():
+                    norm_finish()
+
+                @pl.when(i >= LAG_B)
+                def _():
+                    c = i - LAG_B
+                    r = ratio[...][:, 0:1]
+                    d_b(c).wait_recv()
+                    q = pb[c].astype(f32) + rcv_b[c].astype(f32) + r * q_own[c]
+                    q_own[c] = q
+                    q_all[c] = q.astype(bf16)
+                    d_q(c).start()
+                    qq[...] = qq[...] + lanes(q * q)
+
+                    @pl.when(jnp.logical_not(last))
+                    def _():
+                        back(c)
+
+            each(N + LAG_B, go)
+            send_curv(dq[...] + 0.5 * qq[...])
+
+            def sent(c):
+                d_b(c).wait_send()
+                d_q(c).wait_send()
+
+            each(N, sent)
+
+        @pl.when(last)
         def _():
             curv_forward()
-
-            def arrive(s, c):
-                for j in CJ:
-                    d_agc(j, s).wait_recv()
-                for j in CJ:
-                    d_agc(j, s).wait_send()
-                return c
-
-            lax.fori_loop(0, S, arrive, 0)
             curv_finish()
             advance()
-            lax.fori_loop(0, S, project, 0)
+            each(S, project)
+
+            @pl.when(t < ITERS * CG_STEPS - 1)
+            def _():
+                each(N, back)
 
         return carry
 
@@ -502,10 +556,9 @@
 
     for j in SJ:
         d_fin(j).start()
-    here = pl.ds(pl.multiple_of(mc * RQ, 128), RQ)
     for s in range(S):
-        slack_out[s] = slack[s, :, here]
-        dual_out[s] = dual[s, :, here]
+        slack_out[s] = slack[s * H + mc]
+        dual_out[s] = dual[s * H + mc]
     for j in SJ:
         d_fin(j).wait_recv()
     for j in SJ:
@@ -521,7 +574,8 @@
     B = rhs.shape[0]
     S, R, C1 = tech.shape
     C2 = recourse.shape[2]
-    RQ = R // n_col
+    RH = R // n_col
+    N = S * n_col
     SH = C1 // n_scen
     starts = jnp.concatenate(
         [jnp.ones((S, 1), f32), (cone_id[:, 1:] != cone_id[:, :-1]).astype(f32)], axis=1)
@@ -530,22 +584,21 @@
     V = pltpu.VMEM
     D = pltpu.SemaphoreType.DMA
     ns, nc = n_scen - 1, n_col - 1
+    rows = lambda dt: V((N, B, RH), dt)
     scratch = [
-        V((S, R, C1), bf16), V((S, R, C2), bf16),
-        V((S, B, R), f32), V((S, B, R), f32), V((S, B, R), f32),
-        V((S, NCONE, R), bf16),
-        V((S, n_col, B, RQ), bf16), V((S, n_col, B, RQ), bf16), V((nc, S, B, RQ), bf16),
-        V((S, B, RQ), f32),
+        V((N, RH, C1 + C2), bf16),
+        rows(f32), rows(f32), rows(f32), V((S, NCONE, R), bf16),
+        rows(f32), rows(bf16), rows(bf16), rows(bf16), rows(f32), rows(bf16),
         V((n_scen, B, SH), f32), V((n_scen, B, SH), bf16), V((ns, B, SH), bf16), V((n_scen, B, SH), bf16),
         V((S, B, C2), f32), V((S, B, C2), f32), V((S, B, C2), f32),
         V((B, SH), f32), V((B, SH), f32),
         V((8, 128), f32), V((ns, 8, 128), f32), V((8, 128), f32), V((nc, 8, 128), f32),
         V((8, 128), f32), V((nc, 8, 128), f32), V((8, 128), f32), V((ns, 8, 128), f32),
-        V((B, 128), f32), V((B, 128), f32), V((B, 128), f32), V((B, 128), f32),
+        V((B, 128), f32), V((B, 128), f32), V((B, 128), f32), V((B, 128), f32), V((B, 128), f32),
         V((n_scen, B, SH), f32),
-        D((S,)), D((S,)), D,
+        D((N,)), D((N,)), D((N,)),
         D((ns,)), D((ns,)), D((ns,)), D((ns,)), D((nc,)), D((nc,)),
-        D((nc, S)), D((nc, S)), D((nc, S)), D((nc, S)),
+        D((N,)), D((N,)), D((N,)), D((N,)), D((N,)), D((N,)),
         D((nc,)), D((nc,)), D((ns,)), D((ns,)), D((ns,)), D((ns,)), D((ns,)), D((ns,)),
     ]
     x, y, slack, dual = pl.pallas_call(
@@ -553,8 +606,8 @@
         out_shape=(
             jax.ShapeDtypeStruct((B, C1), f32),
             jax.ShapeDtypeStruct((S, B, C2), f32),
-            jax.ShapeDtypeStruct((S, B, RQ), f32),
-            jax.ShapeDtypeStruct((S, B, RQ), f32),
+            jax.ShapeDtypeStruct((S, B, RH), f32),
+            jax.ShapeDtypeStruct((S, B, RH), f32),
         ),
         in_specs=[hbm, hbm, hbm, vm, vm, vm, vm],
         out_specs=(vm, vm, vm, vm),
@@ -580,7 +633,7 @@
         and batch % 16 == 0
         and 1024 % batch == 0
         and n_scen > 1
-        and n_col > 1
+        and n_col == 4
     )
     run = fused if fits else body
     return run(tech, recourse, rhs, cost_first, cost_second, cone_id)

time: 366 us -> 320 us (0.87)
  Pallas kernels: 354 us -> 308 us
    pallas_call x1, Pallas kernels: 354 us -> 308 us  [fused(): pl.pallas_call(functools.partial(kernel_body, (n_scen, n_col, B, S, R, C1...]
where the time goes in v1:
time: 320 us
  Pallas kernels  308 us (96%)
  local copies, waits for them, and re-layouts  9.68 us (3%)
    pallas_call x1, Pallas kernels, fused(): pl.pallas_call(functools.partial(kernel_body, (n_scen, n_col, B, S, R, C1...  308 us
    unnamed x5, local copies, waits for them, and re-layouts  9.68 us

profile of v1, /device:TPU:0, one launch (start us, length us, event | category | flops | bytes accessed | tf_op | source)
XLA Modules:
  0.0 320.0 jit_solution(17534455944185085394)
XLA Ops:
  0.6 0.9 slice_compare_fusion
  1.6 0.7 pad_convert_fusion.starts
  2.3 2.8 copy.15
  5.1 308.0 %shard_map.93 = (f32[32,1024]{1,0:T(8,128)}, f32[4,32,256]{2,1,0:T(8,128)}, f32[4,32,512]{2,1,0:T(8,128)}, f32[4,32,512]{2,1,0:T(8,128)}) custom-call(bf16[4,2048,1024]{2,1,0:T(8,128)(2,1)} %tech_hbm.1, bf16[4,2048,256]{2,1,0:T(8,128)(2,1)} %rec_hbm.1, f32[4,32,2048]{2,1,0:T(8,128)} %bitcast.7, f32[1,1024]{1,0:T(1,128)} %bitcast.11, f32[4,256]{1,0:T(4,128)} %cost2.1, ...), custom_call_target="tpu_custom_call" | custom-call | tf_op jit(solution)/shard_map/pallas_call | solution.py:604
  313.1 1.6 copy.11
  314.8 1.8 copy.12
  316.6 1.8 copy.13
  318.4 1.6 copy.17

commit v2 on v1

v2 whole, which is shorter than its diff:
```python
import functools

import jax
import jax.numpy as jnp
from jax import lax
from jax.experimental import pallas as pl
from jax.experimental.pallas import tpu as pltpu
from jax.sharding import PartitionSpec as P

NCONE = 128
ITERS = 3
CG_STEPS = 3
CHUNKS = 2
LAG_A = 3
LAG_B = 6
LAG_E = 7


HIGH = lax.Precision.HIGHEST


def cone_factors(lead, tail):
    norm_tail = jnp.sqrt(tail)
    inside = norm_tail <= lead
    polar = norm_tail <= -lead
    safe = jnp.where(norm_tail > 0.0, norm_tail, 1.0)
    middle = 0.5 * (lead + norm_tail)
    head = jnp.where(inside, lead, jnp.where(polar, 0.0, middle))
    scale = jnp.where(inside, 1.0, jnp.where(polar, 0.0, middle / safe))
    return (head, scale)


def body(tech, recourse, rhs, cost_first, cost_second, cone_id):
    f32 = jnp.float32
    bf16 = jnp.bfloat16
    n_scen = lax.axis_size("scen")
    n_col = lax.axis_size("col")
    batch = rhs.shape[0]
    scen_local = tech.shape[0]
    rows = tech.shape[1]
    first_cols = tech.shape[2]
    tech_flat = tech.reshape(scen_local * rows, first_cols)
    starts = jnp.concatenate(
        [jnp.ones((scen_local, 1), f32), (cone_id[:, 1:] != cone_id[:, :-1]).astype(f32)], axis=1
    )
    labels = lax.broadcasted_iota(jnp.int32, (1, 1, NCONE), 2)
    onehot = (cone_id[:, :, None] == labels).astype(f32)
    part_rows = rows // n_col
    row_start = lax.axis_index("col") * part_rows
    row_weight = 1.0 / n_col
    share_cols = first_cols // n_scen
    cost_here = lax.dynamic_slice_in_dim(
        cost_first, lax.axis_index("scen") * share_cols, share_cols, 0
    )
    first_weight = 1.0
    start_rows = starts[None]

    def couple(partial_value):
        return lax.psum_scatter(partial_value, "scen", scatter_dimension=1, tiled=True)

    def adjoint(rows_bf):
        first_part = jnp.dot(
            rows_bf.reshape(batch, scen_local * rows), tech_flat, preferred_element_type=f32
        )
        second_part = jnp.einsum("bsm,smk->bsk", rows_bf, recourse, preferred_element_type=f32)
        return (first_part, second_part)

    def local_squares(first_vec, second_vec):
        return first_weight * jnp.sum(first_vec * first_vec, axis=1) + jnp.sum(
            second_vec * second_vec, axis=(1, 2)
        )

    def total_norm(first_vec, second_vec):
        return lax.psum(local_squares(first_vec, second_vec), ("scen", "col"))

    here_rows = rhs.shape[2]
    first_sol = jnp.zeros((batch, share_cols), f32)
    second_sol = jnp.zeros((batch, scen_local, recourse.shape[2]), f32)
    slack = jnp.zeros((batch, scen_local, here_rows), f32)
    dual = jnp.zeros((batch, scen_local, here_rows), f32)
    image = jnp.zeros((batch, scen_local, here_rows), f32)
    for outer in range(ITERS):
        resid_rows = (rhs - slack - dual - image).astype(bf16)
        back_first, back_second = adjoint(resid_rows)
        res_first = couple(back_first) - cost_here[None, :]
        res_second = back_second - cost_second[None]
        res_norm = total_norm(res_first, res_second)
        dir_first, dir_second = (res_first, res_second)
        for step in range(CG_STEPS):
            dir_first_bf = lax.all_gather(dir_first.astype(bf16), "scen", axis=1, tiled=True)
            forward_partial_value = lax.dot_general(
                dir_first_bf, tech_flat, (((1,), (1,)), ((), ())), preferred_element_type=f32
            )
            forward_partial_value = forward_partial_value.reshape(batch, scen_local, rows)
            image_step = lax.psum(
                forward_partial_value
                + jnp.einsum(
                    "bsk,smk->bsm", dir_second.astype(bf16), recourse, preferred_element_type=f32
                ),
                "col",
            )
            curv_term = local_squares(dir_first, dir_second) + row_weight * jnp.sum(
                image_step * image_step, axis=(1, 2)
            )
            curv = lax.psum(curv_term, ("scen", "col"))
            alpha = res_norm / curv
            first_sol = first_sol + alpha[:, None] * dir_first
            second_sol = second_sol + alpha[:, None, None] * dir_second
            image = image + alpha[:, None, None] * image_step
            if step + 1 < CG_STEPS:
                back_first, back_second = adjoint(image_step.astype(bf16))
                res_first = res_first - alpha[:, None] * (dir_first + couple(back_first))
                res_second = res_second - alpha[:, None, None] * (dir_second + back_second)
                new_norm = total_norm(res_first, res_second)
                ratio = new_norm / res_norm
                dir_first = res_first + ratio[:, None] * dir_first
                dir_second = res_second + ratio[:, None, None] * dir_second
                res_norm = new_norm
        values = rhs - image - dual
        project_lead = jnp.einsum("bsm,smc->bsc", values * start_rows, onehot, precision=HIGH)
        project_tail = jnp.einsum(
            "bsm,smc->bsc", values * values * (1.0 - start_rows), onehot, precision=HIGH
        )
        project_lead, project_tail = (project_lead, project_tail)
        head, scale = cone_factors(project_lead, project_tail)
        head_rows = jnp.einsum("bsc,smc->bsm", head, onehot, precision=HIGH)
        scale_rows = jnp.einsum("bsc,smc->bsm", scale, onehot, precision=HIGH)
        slack = start_rows * head_rows + (1.0 - start_rows) * values * scale_rows
        dual = dual + image + slack - rhs
    first_out = lax.all_gather(first_sol, "scen", axis=1, tiled=True)
    slack_out = lax.dynamic_slice_in_dim(slack, row_start, part_rows, 2)
    dual_out = lax.dynamic_slice_in_dim(dual, row_start, part_rows, 2)
    return (first_out, second_sol, slack_out, dual_out)


def kernel_body(
    dims,
    tech_hbm, rec_hbm, rhs_hbm, cost1, cost2, cid, starts,
    x_out, y_out, slack_out, dual_out,
    wts, wtt, g, dual, slack, onehot, part, pb, rcv_a, rcv_b, u, dz,
    px, acc, bq1, res1, dir1, sol1, xin, bk2, bq2, res2, dir2, sol2,
    sc1, sc2, uu, uv, uw,
    nres, dirn, qn, rat, alphas, rats,
    ld_t, ld_r, ld_g,
    a_s, a_r, b_s, b_r, u_s, u_r, px_s, px_r, c1_s, c1_r, c2_s, c2_r,
):
    n_scen, n_col, B, S, R, C1, C2 = dims
    f32, bf16 = jnp.float32, jnp.bfloat16
    H = CHUNKS
    RH = R // H
    N = S * H
    K = B // 2
    CB = 256
    G = K // 8
    W = 128 // (5 * G)
    TAIL = N // 2
    SLOTS = N + LAG_A
    TURNS = 2 * ITERS * (CG_STEPS + 1)
    ms = lax.axis_index("scen")
    mc = lax.axis_index("col")
    pair = mc + 1 - 2 * lax.rem(mc, 2)
    across = 3 - mc
    is_end = jnp.logical_or(mc == 0, mc == 3)
    is_mid = jnp.logical_or(mc == 1, mc == 2)
    lag = LAG_E - (LAG_E - LAG_B) * lax.rem((mc + 1) // 2, 2)

    def scen_peer(j):
        return lax.rem(ms + j, n_scen)

    def col_peer(j):
        return lax.rem(mc + j, n_col)

    def to_scen(src, dst, ss, rs, j):
        return pltpu.make_async_remote_copy(
            src_ref=src, dst_ref=dst, send_sem=ss, recv_sem=rs,
            device_id=(scen_peer(j), mc), device_id_type=pl.DeviceIdType.MESH)

    def to_col(src, dst, ss, rs, target):
        return pltpu.make_async_remote_copy(
            src_ref=src, dst_ref=dst, send_sem=ss, recv_sem=rs,
            device_id=(ms, target), device_id_type=pl.DeviceIdType.MESH)

    SJ = range(1, n_scen)
    CJ = range(1, n_col)

    def d_a(i, c):
        return to_col(pb.at[i, c], rcv_a.at[i, c], a_s.at[i, c], a_r.at[i, c], pair)

    def d_b(i, c):
        return to_col(pb.at[i, c], rcv_b.at[i, c], b_s.at[i, c], b_r.at[i, c], across)

    def d_u(i, k, c):
        return to_col(u.at[i, k, c], u.at[i, k, c], u_s.at[i, c], u_r.at[i, c], pair)

    def d_px(i, p, j):
        return to_scen(px.at[i, p, ms], px.at[i, p, ms], px_s.at[i, p, j - 1], px_r.at[i, p, j - 1], j)

    def d_c1(i, k, j):
        return to_col(sc1.at[i, k, mc], sc1.at[i, k, mc], c1_s.at[i, k, j - 1], c1_r.at[i, k, j - 1], col_peer(j))

    def d_c2(i, j):
        return to_scen(sc2.at[i, ms], sc2.at[i, ms], c2_s.at[i, j - 1], c2_r.at[i, j - 1], j)

    lane_no = lax.broadcasted_iota(jnp.int32, (8, 128), 1)
    lane_group = lane_no // W

    def pack(parts):
        out = jnp.zeros((8, 128), f32)
        for n, x in enumerate(parts):
            tot = jnp.broadcast_to(jnp.sum(x, axis=1, keepdims=True), (K, 128))
            for k in range(G):
                out = jnp.where(lane_group == n * G + k, tot[8 * k:8 * k + 8], out)
        return out

    def unpack(p):
        return [jnp.concatenate(
            [jnp.broadcast_to(
                jnp.sum(jnp.where(lane_no == W * (n * G + k), p, 0.0), axis=1, keepdims=True), (8, 128))
             for k in range(G)], axis=0) for n in range(5)]

    def lanes(x):
        out = x[:, 0:128]
        for k in range(1, x.shape[1] // 128):
            out = out + x[:, 128 * k:128 * k + 128]
        return out

    def rows_of(c):
        return c // H, pl.ds(pl.multiple_of(lax.rem(c, H) * RH, RH), RH)

    def load_t(c):
        s, rows = rows_of(c)
        return pltpu.make_async_copy(tech_hbm.at[s, rows, :], wts.at[c, :, pl.ds(0, C1)], ld_t.at[c])

    def load_r(c):
        s, rows = rows_of(c)
        return pltpu.make_async_copy(rec_hbm.at[s, rows, :], wts.at[c, :, pl.ds(C1, C2)], ld_r.at[c])

    def load_g(i, c):
        s, rows = rows_of(c)
        return pltpu.make_async_copy(rhs_hbm.at[s, pl.ds(i * K, K), rows], g.at[i, c], ld_g.at[i, c])

    def each(n, f):
        def one(c, carry):
            f(c)
            return carry
        lax.fori_loop(0, n, one, 0)

    def load_all(c):
        load_g(0, c).start()
        load_g(1, c).start()
        load_t(c).start()
        load_r(c).start()

    each(N, load_all)

    barrier = pltpu.get_barrier_semaphore()
    for j in SJ:
        pl.semaphore_signal(barrier, inc=1, device_id=(scen_peer(j), mc), device_id_type=pl.DeviceIdType.MESH)
    for j in CJ:
        pl.semaphore_signal(barrier, inc=1, device_id=(ms, col_peer(j)), device_id_type=pl.DeviceIdType.MESH)

    for ref in (bq1, dir1, sol1, bq2, dir2, sol2, uu, uv, uw, nres, dirn, qn, rat, dual, u, acc, bk2):
        ref[...] = jnp.zeros_like(ref)

    def init_cones(s):
        ids = cid[pl.ds(s, 1), :]
        onehot[s] = (lax.broadcasted_iota(jnp.int32, (NCONE, R), 0) == ids).astype(f32).astype(bf16)

    each(S, init_cones)

    def add_back(i, s, f):
        acc[i] = acc[i] + f[:, 0:C1]
        bk2[i, s] = bk2[i, s] + f[:, C1:C1 + C2]

    def back(i, c, z):
        add_back(i, c // H, jnp.dot(z, wts[c], preferred_element_type=f32))

    def first_back(c):
        load_g(0, c).wait()
        load_g(1, c).wait()
        load_t(c).wait()
        load_r(c).wait()
        z = jnp.concatenate([g[0, c], g[1, c]], axis=0).astype(bf16)
        f = jnp.dot(z, wts[c], preferred_element_type=f32)
        add_back(0, c // H, f[0:K])
        add_back(1, c // H, f[K:2 * K])
        for j in range((C1 + C2) // CB):
            cols = slice(j * CB, (j + 1) * CB)
            wtt[c, cols, :] = wts[c, :, cols].T

    each(N, first_back)
    pl.semaphore_wait(barrier, n_scen + n_col - 2)

    def send_first(i, p):
        px[i, p, ms] = acc[i].astype(bf16)
        for j in SJ:
            d_px(i, p, j).start()

    def take_first(i, p):
        for j in SJ:
            d_px(i, p, j).wait_recv()
        tot = px[i, p, 0].astype(f32)
        for k in range(1, n_scen):
            tot = tot + px[i, p, k].astype(f32)
        for j in SJ:
            d_px(i, p, j).wait_send()
        return tot

    def new_direction(i, k):
        r1 = res1[i]
        xin[i] = r1.astype(bf16)
        sq = lanes(r1 * r1) * (1.0 / n_scen)
        cr = lanes(r1 * dir1[i]) * (1.0 / n_scen)
        for s in range(S):
            r2 = res2[i, s]
            sq = sq + lanes(r2 * r2)
            cr = cr + lanes(r2 * dir2[i, s])
        sc1[i, k, mc] = pack([sq, cr])
        for j in CJ:
            d_c1(i, k, j).start()

    def restart(i):
        res1[i] = take_first(i, 1) - cost1[...]
        for s in range(S):
            res2[i, s] = bk2[i, s] - cost2[s:s + 1, :]
        new_direction(i, 0)

    send_first(0, 1)
    send_first(1, 1)
    restart(0)

    def front(i, c):
        x = jnp.concatenate([xin[i], res2[i, c // H].astype(bf16)], axis=1)
        return jnp.dot(x, wtt[c], preferred_element_type=f32)

    def relay(i, c):
        d_a(i, c).wait_recv()
        pb[i, c] = (part[c] + rcv_a[i, c].astype(f32)).astype(bf16)
        d_b(i, c).start()

    def finish_rows(i, k, c):
        @pl.when(is_end)
        def _():
            d_u(i, k, c).wait_recv()

        @pl.when(is_mid)
        def _():
            d_b(i, c).wait_recv()
            u[i, k, c] = (pb[i, c].astype(f32) + rcv_b[i, c].astype(f32)).astype(bf16)
            d_u(i, k, c).start()

        v = u[i, k, c].astype(f32)
        before = u[i, lax.rem(k + CG_STEPS - 1, CG_STEPS), c].astype(f32)
        earlier = u[i, lax.rem(k + CG_STEPS - 2, CG_STEPS), c].astype(f32)
        uu[i] = uu[i] + lanes(v * v)
        uv[i] = uv[i] + lanes(v * before)
        uw[i] = uw[i] + lanes(v * earlier)

    def send_scalars(i, k):
        total = pack([jnp.zeros((K, 128), f32)] * 2 + [uu[i], uv[i], uw[i]])
        for j in CJ:
            d_c1(i, k, j).wait_recv()
        for m in range(n_col):
            total = total + sc1[i, k, m]
        for j in CJ:
            d_c1(i, k, j).wait_send()
        sc2[i, ms] = total
        for j in SJ:
            d_c2(i, j).start()

    def finish_scalars(i, k):
        for j in SJ:
            d_c2(i, j).wait_recv()
        total = sc2[i, 0]
        for m in range(1, n_scen):
            total = total + sc2[i, m]
        for j in SJ:
            d_c2(i, j).wait_send()
        s0, s1, s2, s3, s4 = unpack(total)
        r = jnp.where(k == 0, 0.0, s0 / nres[i])
        dn = s0 + r * (2.0 * s1 + r * dirn[i])
        qs = s2 + r * (2.0 * (s3 + rat[i] * s4) + r * qn[i])
        nres[i] = s0
        dirn[i] = dn
        qn[i] = qs
        rat[i] = r
        rats[i, k] = r
        a = s0 / (dn + qs)
        alphas[i, k] = a
        r, a = r[:, 0:1], a[:, 0:1]
        d1 = res1[i] + r * dir1[i]
        dir1[i] = d1
        sol1[i] = sol1[i] + a * d1
        for s in range(S):
            d2 = res2[i, s] + r * dir2[i, s]
            dir2[i, s] = d2
            sol2[i, s] = sol2[i, s] + a * d2

    def next_residual(i, k):
        r, a = rats[i, k][:, 0:1], alphas[i, k][:, 0:1]
        q1 = take_first(i, lax.rem(k, 2)) + r * bq1[i]
        bq1[i] = q1
        res1[i] = res1[i] - a * (dir1[i] + q1)
        for s in range(S):
            q2 = bk2[i, s] + r * bq2[i, s]
            bq2[i, s] = q2
            res2[i, s] = res2[i, s] - a * (dir2[i, s] + q2)
        new_direction(i, k + 1)

    def all_sent(i, k):
        @pl.when(is_end)
        def _():
            each(N, lambda c: d_a(i, c).wait_send())

        @pl.when(is_mid)
        def _():
            def one(c):
                d_b(i, c).wait_send()
                d_u(i, k, c).wait_send()

            each(N, one)

    def split(x):
        hi = x.astype(bf16)
        return [hi, (x - hi.astype(f32)).astype(bf16)]

    def project(i):
        c2 = alphas[i, 2]
        c1 = alphas[i, 1] + rats[i, 2] * c2
        c0 = alphas[i, 0] + rats[i, 1] * c1
        c0, c1, c2 = c0[:, 0:1], c1[:, 0:1], c2[:, 0:1]

        def one(s):
            st = starts[pl.ds(s, 1), :]
            pieces = []
            for h in range(H):
                c = s * H + h
                piece = g[i, c] - (c0 * u[i, 0, c].astype(f32) + c1 * u[i, 1, c].astype(f32)
                                   + c2 * u[i, 2, c].astype(f32))
                g[i, c] = piece
                pieces.append(piece)
            gs = jnp.concatenate(pieces, axis=1)
            v = gs - jnp.concatenate([dual[i, s * H + h] for h in range(H)], axis=1)
            lead_v = v * st
            tail_v = v * v * (1.0 - st)
            stack = jnp.concatenate(split(lead_v) + split(tail_v), axis=0)
            sums = lax.dot_general(stack, onehot[s], (((1,), (1,)), ((), ())), preferred_element_type=f32)
            lead = sums[0:K] + sums[K:2 * K]
            tail = sums[2 * K:3 * K] + sums[3 * K:4 * K]
            head, scale = cone_factors(lead, tail)
            stack2 = jnp.concatenate(split(head) + split(scale), axis=0)
            outs = jnp.dot(stack2, onehot[s], preferred_element_type=f32)
            head_rows = outs[0:K] + outs[K:2 * K]
            scale_rows = outs[2 * K:3 * K] + outs[3 * K:4 * K]
            sl = st * head_rows + (1.0 - st) * v * scale_rows
            du = sl - v
            d = (gs - sl - du).astype(bf16)
            for h in range(H):
                cols = slice(h * RH, (h + 1) * RH)
                slack[i, s * H + h] = sl[:, cols]
                dual[i, s * H + h] = du[:, cols]
                dz[s * H + h] = d[:, cols]

        each(S, one)

    def turn(t, carry):
        a = lax.rem(t, 2)
        b = 1 - a
        ka = lax.rem(t // 2, CG_STEPS + 1)
        kb = lax.rem((t + 2 * CG_STEPS + 1) // 2, CG_STEPS + 1)
        run_a, run_b = ka < CG_STEPS, kb < CG_STEPS
        back_a, back_b = ka < CG_STEPS - 1, kb < CG_STEPS - 1
        acc[a] = jnp.zeros((K, C1), f32)
        bk2[a] = jnp.zeros((S, K, C2), f32)
        uu[a] = jnp.zeros((K, 128), f32)
        uv[a] = jnp.zeros((K, 128), f32)
        uw[a] = jnp.zeros((K, 128), f32)

        def slot(k):
            @pl.when(jnp.logical_and(run_a, k < N))
            def _():
                p = front(a, k)

                @pl.when(is_end)
                def _():
                    pb[a, k] = p.astype(bf16)
                    d_a(a, k).start()

                @pl.when(is_mid)
                def _():
                    part[k] = p

            @pl.when(jnp.logical_and(run_b, k < TAIL))
            def _():
                c = N - TAIL + k
                finish_rows(b, kb, c)

                @pl.when(back_b)
                def _():
                    back(b, c, u[b, kb, c])

                @pl.when(k == TAIL - 1)
                def _():
                    @pl.when(back_b)
                    def _():
                        send_first(b, lax.rem(kb, 2))

                    send_scalars(b, kb)

            @pl.when(jnp.logical_and(jnp.logical_and(run_a, is_mid), k >= LAG_A))
            def _():
                relay(a, k - LAG_A)

            @pl.when(jnp.logical_and(run_a, jnp.logical_and(k >= lag, k < lag + N - TAIL)))
            def _():
                c = k - lag
                finish_rows(a, ka, c)

                @pl.when(back_a)
                def _():
                    back(a, c, u[a, ka, c])

        each(SLOTS, slot)

        @pl.when(ka == CG_STEPS)
        def _():
            project(a)

            @pl.when(t < TURNS - 2)
            def _():
                each(N, lambda c: back(a, c, dz[c]))
                send_first(a, 1)

        @pl.when(run_b)
        def _():
            finish_scalars(b, kb)
            all_sent(b, kb)

        @pl.when(back_b)
        def _():
            next_residual(b, kb)

        @pl.when(jnp.logical_and(kb == CG_STEPS, t < TURNS - 1))
        def _():
            restart(b)

        return carry

    lax.fori_loop(0, TURNS, turn, 0)

    RQ = R // n_col
    own = mc * RQ // RH
    here = pl.ds(pl.multiple_of(lax.rem(mc * RQ, RH), 128), RQ)
    for i in range(2):
        rows = slice(i * K, (i + 1) * K)
        x_out[rows, :] = sol1[i]
        for s in range(S):
            y_out[s, rows, :] = sol2[i, s]
            slack_out[s, rows, :] = slack[i, s * H + own, :, here]
            dual_out[s, rows, :] = dual[i, s * H + own, :, here]


def fused(tech, recourse, rhs, cost_first, cost_second, cone_id):
    f32, bf16 = jnp.float32, jnp.bfloat16
    n_scen = lax.axis_size("scen")
    n_col = lax.axis_size("col")
    B = rhs.shape[0]
    S, R, C1 = tech.shape
    C2 = recourse.shape[2]
    RQ = R // n_col
    RH = R // CHUNKS
    N = S * CHUNKS
    K = B // 2
    starts = jnp.concatenate(
        [jnp.ones((S, 1), f32), (cone_id[:, 1:] != cone_id[:, :-1]).astype(f32)], axis=1)
    vm = pl.BlockSpec(memory_space=pltpu.VMEM)
    hbm = pl.BlockSpec(memory_space=pl.ANY)
    V = pltpu.VMEM
    D = pltpu.SemaphoreType.DMA
    ns, nc = n_scen - 1, n_col - 1
    rows = lambda dt: V((2, N, K, RH), dt)
    one = V((2, K, C1), f32)
    two = V((2, S, K, C2), f32)
    num = V((2, K, 128), f32)
    scratch = [
        V((N, RH, C1 + C2), bf16), V((N, C1 + C2, RH), bf16),
        rows(f32), rows(f32), rows(f32), V((S, NCONE, R), bf16), V((N, K, RH), f32),
        rows(bf16), rows(bf16), rows(bf16), V((2, CG_STEPS, N, K, RH), bf16), V((N, K, RH), bf16),
        V((2, 2, n_scen, K, C1), bf16), one, one, one, one, one, V((2, K, C1), bf16),
        two, two, two, two, two,
        V((2, CG_STEPS, n_col, 8, 128), f32), V((2, n_scen, 8, 128), f32), num, num, num,
        num, num, num, num, V((2, CG_STEPS, K, 128), f32), V((2, CG_STEPS, K, 128), f32),
        D((N,)), D((N,)), D((2, N)),
        D((2, N)), D((2, N)), D((2, N)), D((2, N)), D((2, N)), D((2, N)),
        D((2, 2, ns)), D((2, 2, ns)), D((2, CG_STEPS, nc)), D((2, CG_STEPS, nc)), D((2, ns)), D((2, ns)),
    ]
    x, y, slack, dual = pl.pallas_call(
        functools.partial(kernel_body, (n_scen, n_col, B, S, R, C1, C2)),
        out_shape=(
            jax.ShapeDtypeStruct((B, C1), f32),
            jax.ShapeDtypeStruct((S, B, C2), f32),
            jax.ShapeDtypeStruct((S, B, RQ), f32),
            jax.ShapeDtypeStruct((S, B, RQ), f32),
        ),
        in_specs=[hbm, hbm, hbm, vm, vm, vm, vm],
        out_specs=(vm, vm, vm, vm),
        scratch_shapes=scratch,
        compiler_params=pltpu.CompilerParams(
            collective_id=0, has_side_effects=True, vmem_limit_bytes=62 * 1024 * 1024),
    )(
        tech, recourse, jnp.transpose(rhs, (1, 0, 2)),
        cost_first.reshape(1, C1), cost_second, cone_id, starts,
    )
    back = lambda a: jnp.transpose(a, (1, 0, 2))
    return x, back(y), back(slack), back(dual)


def program(tech, recourse, rhs, cost_first, cost_second, cone_id):
    n_scen = lax.axis_size("scen")
    n_col = lax.axis_size("col")
    batch = rhs.shape[0]
    fits = (
        (tech.shape[2] + recourse.shape[2]) % 256 == 0
        and tech.shape[2] % (128 * n_scen) == 0
        and tech.shape[1] % (128 * n_col) == 0
        and recourse.shape[2] % 128 == 0
        and batch % 32 == 0
        and batch <= 256
        and n_scen > 1
        and n_col == 4
    )
    run = fused if fits else body
    return run(tech, recourse, rhs, cost_first, cost_second, cone_id)


def solution(mesh):
    placed = (
        P("scen", None, "col"),
        P("scen", None, "col"),
        P(None, "scen", None),
        P("col"),
        P("scen", "col"),
        P("scen", None),
    )
    return jax.shard_map(
        program,
        mesh=mesh,
        in_specs=placed,
        out_specs=(
            P(None, "col"),
            P(None, "scen", "col"),
            P(None, "scen", "col"),
            P(None, "scen", "col"),
        ),
        check_vma=False,
    )
```

time: 320 us -> 309 us (0.966)
  Pallas kernels: 308 us -> 296 us
    pallas_call x1, Pallas kernels: 308 us -> 296 us  [fused(): pl.pallas_call(functools.partial(kernel_body, (n_scen, n_col, B, S, R, C1...]
where the time goes in v2:
time: 309 us; the launch traced here: 308 us
  Pallas kernels  296 us (96%)
  local copies, waits for them, and re-layouts  9.68 us (3%)
    pallas_call x1, Pallas kernels, fused(): pl.pallas_call(functools.partial(kernel_body, (n_scen, n_col, B, S, R, C1...  296 us
    unnamed x5, local copies, waits for them, and re-layouts  9.68 us

profile of v2, /device:TPU:0, one launch (start us, length us, event | category | flops | bytes accessed | tf_op | source)
XLA Modules:
  0.0 308.3 jit_solution(16748936472059926965)
XLA Ops:
  0.6 0.9 slice_compare_fusion
  1.6 0.7 pad_convert_fusion.starts
  2.3 2.8 copy.15
  5.1 296.3 %shard_map.93 = (f32[32,1024]{1,0:T(8,128)}, f32[4,32,256]{2,1,0:T(8,128)}, f32[4,32,512]{2,1,0:T(8,128)}, f32[4,32,512]{2,1,0:T(8,128)}) custom-call(bf16[4,2048,1024]{2,1,0:T(8,128)(2,1)} %tech_hbm.1, bf16[4,2048,256]{2,1,0:T(8,128)(2,1)} %rec_hbm.1, f32[4,32,2048]{2,1,0:T(8,128)} %bitcast.7, f32[1,1024]{1,0:T(1,128)} %bitcast.11, f32[4,256]{1,0:T(4,128)} %cost2.1, ...), custom_call_target="tpu_custom_call" | custom-call | tf_op jit(solution)/shard_map/pallas_call | solution.py:597
  301.4 1.6 copy.11
  303.1 1.8 copy.12
  304.9 1.8 copy.13
  306.7 1.6 copy.17

commit v3 on v2

--- a/solution.py
+++ b/solution.py
@@ -11,9 +11,13 @@
 ITERS = 3
 CG_STEPS = 3
 CHUNKS = 2
-LAG_A = 3
-LAG_B = 6
+LAG_A = 4
+LAG_B = 7
 LAG_E = 7
+TAIL_M = 3
+TAIL_E = 6
+FROM_M = 0
+FROM_E = 0
 
 
 HIGH = lax.Precision.HIGHEST
@@ -135,7 +139,7 @@
 
 def kernel_body(
     dims,
-    tech_hbm, rec_hbm, rhs_hbm, cost1, cost2, cid, starts,
+    tech_hbm, rec_hbm, rhs_hbm, cost1, cost2, cid,
     x_out, y_out, slack_out, dual_out,
     wts, wtt, g, dual, slack, onehot, part, pb, rcv_a, rcv_b, u, dz,
     px, acc, bq1, res1, dir1, sol1, xin, bk2, bq2, res2, dir2, sol2,
@@ -153,8 +157,7 @@
     CB = 256
     G = K // 8
     W = 128 // (5 * G)
-    TAIL = N // 2
-    SLOTS = N + LAG_A
+    SLOTS = max(N + LAG_A, LAG_B + N - TAIL_M, LAG_E + N - TAIL_E)
     TURNS = 2 * ITERS * (CG_STEPS + 1)
     ms = lax.axis_index("scen")
     mc = lax.axis_index("col")
@@ -162,10 +165,18 @@
     across = 3 - mc
     is_end = jnp.logical_or(mc == 0, mc == 3)
     is_mid = jnp.logical_or(mc == 1, mc == 2)
-    lag = LAG_E - (LAG_E - LAG_B) * lax.rem((mc + 1) // 2, 2)
+    mid = lax.rem((mc + 1) // 2, 2)
+    lag = LAG_E + (LAG_B - LAG_E) * mid
+    tail = TAIL_E + (TAIL_M - TAIL_E) * mid
+    tail_from = FROM_E + (FROM_M - FROM_E) * mid
+    project_from = TAIL_M * mid
 
     def scen_peer(j):
-        return lax.rem(ms + j, n_scen)
+        out = 0
+        for bit in range(n_scen.bit_length() - 1):
+            own = lax.rem(ms // (1 << bit), 2)
+            out = out + (1 << bit) * (1 - own if j >> bit & 1 else own)
+        return out
 
     def col_peer(j):
         return lax.rem(mc + j, n_col)
@@ -180,7 +191,7 @@
             src_ref=src, dst_ref=dst, send_sem=ss, recv_sem=rs,
             device_id=(ms, target), device_id_type=pl.DeviceIdType.MESH)
 
-    SJ = range(1, n_scen)
+    SJ = sorted(range(1, n_scen), key=lambda j: -bin(j >> 1).count("1"))
     CJ = range(1, n_col)
 
     def d_a(i, c):
@@ -237,7 +248,7 @@
 
     def load_g(i, c):
         s, rows = rows_of(c)
-        return pltpu.make_async_copy(rhs_hbm.at[s, pl.ds(i * K, K), rows], g.at[i, c], ld_g.at[i, c])
+        return pltpu.make_async_copy(rhs_hbm.at[pl.ds(i * K, K), s, rows], g.at[i, c], ld_g.at[i, c])
 
     def each(n, f):
         def one(c, carry):
@@ -306,9 +317,8 @@
             d_px(i, p, j).wait_send()
         return tot
 
-    def new_direction(i, k):
+    def send_norms(i, k):
         r1 = res1[i]
-        xin[i] = r1.astype(bf16)
         sq = lanes(r1 * r1) * (1.0 / n_scen)
         cr = lanes(r1 * dir1[i]) * (1.0 / n_scen)
         for s in range(S):
@@ -320,10 +330,11 @@
             d_c1(i, k, j).start()
 
     def restart(i):
-        res1[i] = take_first(i, 1) - cost1[...]
+        r1 = take_first(i, 1) - cost1[...]
+        res1[i] = r1
+        xin[i] = r1.astype(bf16)
         for s in range(S):
             res2[i, s] = bk2[i, s] - cost2[s:s + 1, :]
-        new_direction(i, 0)
 
     send_first(0, 1)
     send_first(1, 1)
@@ -400,12 +411,13 @@
         r, a = rats[i, k][:, 0:1], alphas[i, k][:, 0:1]
         q1 = take_first(i, lax.rem(k, 2)) + r * bq1[i]
         bq1[i] = q1
-        res1[i] = res1[i] - a * (dir1[i] + q1)
+        r1 = res1[i] - a * (dir1[i] + q1)
+        res1[i] = r1
+        xin[i] = r1.astype(bf16)
         for s in range(S):
             q2 = bk2[i, s] + r * bq2[i, s]
             bq2[i, s] = q2
             res2[i, s] = res2[i, s] - a * (dir2[i, s] + q2)
-        new_direction(i, k + 1)
 
     def all_sent(i, k):
         @pl.when(is_end)
@@ -424,44 +436,42 @@
         hi = x.astype(bf16)
         return [hi, (x - hi.astype(f32)).astype(bf16)]
 
-    def project(i):
+    def project(i, s):
         c2 = alphas[i, 2]
         c1 = alphas[i, 1] + rats[i, 2] * c2
         c0 = alphas[i, 0] + rats[i, 1] * c1
         c0, c1, c2 = c0[:, 0:1], c1[:, 0:1], c2[:, 0:1]
-
-        def one(s):
-            st = starts[pl.ds(s, 1), :]
-            pieces = []
-            for h in range(H):
-                c = s * H + h
-                piece = g[i, c] - (c0 * u[i, 0, c].astype(f32) + c1 * u[i, 1, c].astype(f32)
-                                   + c2 * u[i, 2, c].astype(f32))
-                g[i, c] = piece
-                pieces.append(piece)
-            gs = jnp.concatenate(pieces, axis=1)
-            v = gs - jnp.concatenate([dual[i, s * H + h] for h in range(H)], axis=1)
-            lead_v = v * st
-            tail_v = v * v * (1.0 - st)
-            stack = jnp.concatenate(split(lead_v) + split(tail_v), axis=0)
-            sums = lax.dot_general(stack, onehot[s], (((1,), (1,)), ((), ())), preferred_element_type=f32)
-            lead = sums[0:K] + sums[K:2 * K]
-            tail = sums[2 * K:3 * K] + sums[3 * K:4 * K]
-            head, scale = cone_factors(lead, tail)
-            stack2 = jnp.concatenate(split(head) + split(scale), axis=0)
-            outs = jnp.dot(stack2, onehot[s], preferred_element_type=f32)
-            head_rows = outs[0:K] + outs[K:2 * K]
-            scale_rows = outs[2 * K:3 * K] + outs[3 * K:4 * K]
-            sl = st * head_rows + (1.0 - st) * v * scale_rows
-            du = sl - v
-            d = (gs - sl - du).astype(bf16)
-            for h in range(H):
-                cols = slice(h * RH, (h + 1) * RH)
-                slack[i, s * H + h] = sl[:, cols]
-                dual[i, s * H + h] = du[:, cols]
-                dz[s * H + h] = d[:, cols]
-
-        each(S, one)
+        ids = cid[pl.ds(s, 1), :]
+        first = lax.broadcasted_iota(jnp.int32, (1, R), 1) == 0
+        st = jnp.where(jnp.logical_or(first, ids != pltpu.roll(ids, 1, 1)), 1.0, 0.0)
+        pieces = []
+        for h in range(H):
+            c = s * H + h
+            piece = g[i, c] - (c0 * u[i, 0, c].astype(f32) + c1 * u[i, 1, c].astype(f32)
+                               + c2 * u[i, 2, c].astype(f32))
+            g[i, c] = piece
+            pieces.append(piece)
+        gs = jnp.concatenate(pieces, axis=1)
+        v = gs - jnp.concatenate([dual[i, s * H + h] for h in range(H)], axis=1)
+        lead_v = v * st
+        tail_v = v * v * (1.0 - st)
+        stack = jnp.concatenate(split(lead_v) + split(tail_v), axis=0)
+        sums = lax.dot_general(stack, onehot[s], (((1,), (1,)), ((), ())), preferred_element_type=f32)
+        lead = sums[0:K] + sums[K:2 * K]
+        tail = sums[2 * K:3 * K] + sums[3 * K:4 * K]
+        head, scale = cone_factors(lead, tail)
+        stack2 = jnp.concatenate(split(head) + split(scale), axis=0)
+        outs = jnp.dot(stack2, onehot[s], preferred_element_type=f32)
+        head_rows = outs[0:K] + outs[K:2 * K]
+        scale_rows = outs[2 * K:3 * K] + outs[3 * K:4 * K]
+        sl = st * head_rows + (1.0 - st) * v * scale_rows
+        du = sl - v
+        d = (gs - sl - du).astype(bf16)
+        for h in range(H):
+            cols = slice(h * RH, (h + 1) * RH)
+            slack[i, s * H + h] = sl[:, cols]
+            dual[i, s * H + h] = du[:, cols]
+            dz[s * H + h] = d[:, cols]
 
     def turn(t, carry):
         a = lax.rem(t, 2)
@@ -490,28 +500,36 @@
                 def _():
                     part[k] = p
 
-            @pl.when(jnp.logical_and(run_b, k < TAIL))
+            @pl.when(jnp.logical_and(run_a, k == 1))
             def _():
-                c = N - TAIL + k
+                send_norms(a, ka)
+
+            @pl.when(jnp.logical_and(jnp.logical_not(run_a), jnp.logical_and(k >= project_from, k < project_from + S)))
+            def _():
+                project(a, k - project_from)
+
+            @pl.when(jnp.logical_and(run_b, jnp.logical_and(k >= tail_from, k < tail_from + tail)))
+            def _():
+                c = N - tail + k - tail_from
                 finish_rows(b, kb, c)
+
+                @pl.when(k == tail_from + tail - 1)
+                def _():
+                    send_scalars(b, kb)
 
                 @pl.when(back_b)
                 def _():
                     back(b, c, u[b, kb, c])
 
-                @pl.when(k == TAIL - 1)
-                def _():
-                    @pl.when(back_b)
+                    @pl.when(k == tail_from + tail - 1)
                     def _():
                         send_first(b, lax.rem(kb, 2))
 
-                    send_scalars(b, kb)
-
-            @pl.when(jnp.logical_and(jnp.logical_and(run_a, is_mid), k >= LAG_A))
+            @pl.when(jnp.logical_and(jnp.logical_and(run_a, is_mid), jnp.logical_and(k >= LAG_A, k < LAG_A + N)))
             def _():
                 relay(a, k - LAG_A)
 
-            @pl.when(jnp.logical_and(run_a, jnp.logical_and(k >= lag, k < lag + N - TAIL)))
+            @pl.when(jnp.logical_and(run_a, jnp.logical_and(k >= lag, k < lag + N - tail)))
             def _():
                 c = k - lag
                 finish_rows(a, ka, c)
@@ -524,8 +542,6 @@
 
         @pl.when(ka == CG_STEPS)
         def _():
-            project(a)
-
             @pl.when(t < TURNS - 2)
             def _():
                 each(N, lambda c: back(a, c, dz[c]))
@@ -558,6 +574,14 @@
             y_out[s, rows, :] = sol2[i, s]
             slack_out[s, rows, :] = slack[i, s * H + own, :, here]
             dual_out[s, rows, :] = dual[i, s * H + own, :, here]
+
+
+def lay_out(x, y, slack, dual, x_out, y_out, slack_out, dual_out):
+    x_out[...] = x[...]
+    for s in range(y.shape[0]):
+        y_out[:, s, :] = y[s]
+        slack_out[:, s, :] = slack[s]
+        dual_out[:, s, :] = dual[s]
 
 
 def fused(tech, recourse, rhs, cost_first, cost_second, cone_id):
@@ -571,8 +595,6 @@
     RH = R // CHUNKS
     N = S * CHUNKS
     K = B // 2
-    starts = jnp.concatenate(
-        [jnp.ones((S, 1), f32), (cone_id[:, 1:] != cone_id[:, :-1]).astype(f32)], axis=1)
     vm = pl.BlockSpec(memory_space=pltpu.VMEM)
     hbm = pl.BlockSpec(memory_space=pl.ANY)
     V = pltpu.VMEM
@@ -602,17 +624,26 @@
             jax.ShapeDtypeStruct((S, B, RQ), f32),
             jax.ShapeDtypeStruct((S, B, RQ), f32),
         ),
-        in_specs=[hbm, hbm, hbm, vm, vm, vm, vm],
+        in_specs=[hbm, hbm, hbm, vm, vm, vm],
         out_specs=(vm, vm, vm, vm),
         scratch_shapes=scratch,
         compiler_params=pltpu.CompilerParams(
             collective_id=0, has_side_effects=True, vmem_limit_bytes=62 * 1024 * 1024),
     )(
-        tech, recourse, jnp.transpose(rhs, (1, 0, 2)),
-        cost_first.reshape(1, C1), cost_second, cone_id, starts,
+        tech, recourse, rhs,
+        cost_first.reshape(1, C1), cost_second, cone_id,
     )
-    back = lambda a: jnp.transpose(a, (1, 0, 2))
-    return x, back(y), back(slack), back(dual)
+    return pl.pallas_call(
+        lay_out,
+        out_shape=(
+            jax.ShapeDtypeStruct((B, C1), f32),
+            jax.ShapeDtypeStruct((B, S, C2), f32),
+            jax.ShapeDtypeStruct((B, S, RQ), f32),
+            jax.ShapeDtypeStruct((B, S, RQ), f32),
+        ),
+        in_specs=[vm, vm, vm, vm],
+        out_specs=(vm, vm, vm, vm),
+    )(x, y, slack, dual)
 
 
 def program(tech, recourse, rhs, cost_first, cost_second, cone_id):
@@ -626,7 +657,7 @@
         and recourse.shape[2] % 128 == 0
         and batch % 32 == 0
         and batch <= 256
-        and n_scen > 1
+        and n_scen in (2, 4, 8, 16, 32)
         and n_col == 4
     )
     run = fused if fits else body

time: 309 us -> 274 us (0.89)
  Pallas kernels: 296 us -> 273 us
  local copies, waits for them, and re-layouts: 9.68 us -> 0 us
    pallas_call x1, Pallas kernels: 296 us -> 271 us  [fused(): pl.pallas_call(functools.partial(kernel_body, (n_scen, n_col, B, S, R, C1...]
    unnamed x5 -> x0, local copies, waits for them, and re-layouts: 9.68 us -> none
where the time goes in v3:
time: 274 us
  Pallas kernels  273 us (100%)
    pallas_call x1, Pallas kernels, fused(): pl.pallas_call(functools.partial(kernel_body, (n_scen, n_col, B, S, R, C1...  271 us

profile of v3, /device:TPU:0, one launch (start us, length us, event | category | flops | bytes accessed | tf_op | source)
XLA Modules:
  0.0 273.5 jit_solution(14158441783178731381)
XLA Ops:
  0.6 270.8 %shard_map.93 = (f32[32,1024]{1,0:T(8,128)}, f32[4,32,256]{2,1,0:T(8,128)}, f32[4,32,512]{2,1,0:T(8,128)}, f32[4,32,512]{2,1,0:T(8,128)}) custom-call(bf16[4,2048,1024]{2,1,0:T(8,128)(2,1)} %tech_hbm.1, bf16[4,2048,256]{2,1,0:T(8,128)(2,1)} %rec_hbm.1, f32[32,4,2048]{2,1,0:T(4,128)} %rhs_hbm.1, f32[1,1024]{1,0:T(1,128)} %bitcast.1, f32[4,256]{1,0:T(4,128)} %cost2.1, ...), custom_call_target="tpu_custom_call" | custom-call | tf_op jit(solution)/shard_map/pallas_call | solution.py:619
  271.4 2.1 shard_map.94

commit v4 on v3

--- a/solution.py
+++ b/solution.py
@@ -11,13 +11,11 @@
 ITERS = 3
 CG_STEPS = 3
 CHUNKS = 2
-LAG_A = 4
-LAG_B = 7
+LAG_A = 3
+LAG_B = 6
 LAG_E = 7
 TAIL_M = 3
-TAIL_E = 6
-FROM_M = 0
-FROM_E = 0
+TAIL_E = 7
 
 
 HIGH = lax.Precision.HIGHEST
@@ -168,7 +166,6 @@
     mid = lax.rem((mc + 1) // 2, 2)
     lag = LAG_E + (LAG_B - LAG_E) * mid
     tail = TAIL_E + (TAIL_M - TAIL_E) * mid
-    tail_from = FROM_E + (FROM_M - FROM_E) * mid
     project_from = TAIL_M * mid
 
     def scen_peer(j):
@@ -486,20 +483,20 @@
         uv[a] = jnp.zeros((K, 128), f32)
         uw[a] = jnp.zeros((K, 128), f32)
 
+        def keep_front(c):
+            p = front(a, c)
+            part[c] = p
+            pb[a, c] = p.astype(bf16)
+
+        @pl.when(run_a)
+        def _():
+            keep_front(0)
+
+            @pl.when(is_end)
+            def _():
+                d_a(a, 0).start()
+
         def slot(k):
-            @pl.when(jnp.logical_and(run_a, k < N))
-            def _():
-                p = front(a, k)
-
-                @pl.when(is_end)
-                def _():
-                    pb[a, k] = p.astype(bf16)
-                    d_a(a, k).start()
-
-                @pl.when(is_mid)
-                def _():
-                    part[k] = p
-
             @pl.when(jnp.logical_and(run_a, k == 1))
             def _():
                 send_norms(a, ka)
@@ -508,22 +505,40 @@
             def _():
                 project(a, k - project_from)
 
-            @pl.when(jnp.logical_and(run_b, jnp.logical_and(k >= tail_from, k < tail_from + tail)))
-            def _():
-                c = N - tail + k - tail_from
+            ends_tail = k == tail - 1
+            in_tail = jnp.logical_and(run_b, k < tail)
+            in_front = jnp.logical_and(run_a, k + 1 < N)
+            both = jnp.logical_and(jnp.logical_and(in_front, in_tail), back_b)
+            c = jnp.minimum(N - tail + k, N - 1)
+
+            @pl.when(in_tail)
+            def _():
                 finish_rows(b, kb, c)
 
-                @pl.when(k == tail_from + tail - 1)
+                @pl.when(ends_tail)
                 def _():
                     send_scalars(b, kb)
 
-                @pl.when(back_b)
-                def _():
-                    back(b, c, u[b, kb, c])
-
-                    @pl.when(k == tail_from + tail - 1)
-                    def _():
-                        send_first(b, lax.rem(kb, 2))
+            @pl.when(both)
+            def _():
+                keep_front(k + 1)
+                back(b, c, u[b, kb, c])
+
+            @pl.when(jnp.logical_and(in_front, jnp.logical_not(both)))
+            def _():
+                keep_front(k + 1)
+
+            @pl.when(jnp.logical_and(jnp.logical_and(in_tail, back_b), jnp.logical_not(both)))
+            def _():
+                back(b, c, u[b, kb, c])
+
+            @pl.when(jnp.logical_and(in_front, is_end))
+            def _():
+                d_a(a, k + 1).start()
+
+            @pl.when(jnp.logical_and(jnp.logical_and(in_tail, back_b), ends_tail))
+            def _():
+                send_first(b, lax.rem(kb, 2))
 
             @pl.when(jnp.logical_and(jnp.logical_and(run_a, is_mid), jnp.logical_and(k >= LAG_A, k < LAG_A + N)))
             def _():
@@ -544,7 +559,11 @@
         def _():
             @pl.when(t < TURNS - 2)
             def _():
-                each(N, lambda c: back(a, c, dz[c]))
+                def pair_back(n):
+                    back(a, 2 * n, dz[2 * n])
+                    back(a, 2 * n + 1, dz[2 * n + 1])
+
+                each(N // 2, pair_back)
                 send_first(a, 1)
 
         @pl.when(run_b)

time: 274 us -> 267 us (0.974)
  Pallas kernels: 273 us -> 266 us
    pallas_call x1, Pallas kernels: 271 us -> 264 us  [fused(): pl.pallas_call(functools.partial(kernel_body, (n_scen, n_col, B, S, R, C1...]
where the time goes in v4:
time: 267 us; the launch traced here: 266 us
  Pallas kernels  266 us (100%)
    pallas_call x1, Pallas kernels, fused(): pl.pallas_call(functools.partial(kernel_body, (n_scen, n_col, B, S, R, C1...  264 us

profile of v4, /device:TPU:0, one launch (start us, length us, event | category | flops | bytes accessed | tf_op | source)
XLA Modules:
  0.0 266.3 jit_solution(17432362988404099814)
XLA Ops:
  0.6 263.6 %shard_map.93 = (f32[32,1024]{1,0:T(8,128)}, f32[4,32,256]{2,1,0:T(8,128)}, f32[4,32,512]{2,1,0:T(8,128)}, f32[4,32,512]{2,1,0:T(8,128)}) custom-call(bf16[4,2048,1024]{2,1,0:T(8,128)(2,1)} %tech_hbm.1, bf16[4,2048,256]{2,1,0:T(8,128)(2,1)} %rec_hbm.1, f32[32,4,2048]{2,1,0:T(4,128)} %rhs_hbm.1, f32[1,1024]{1,0:T(1,128)} %bitcast.1, f32[4,256]{1,0:T(4,128)} %cost2.1, ...), custom_call_target="tpu_custom_call" | custom-call | tf_op jit(solution)/shard_map/pallas_call | solution.py:638
  264.2 2.1 shard_map.94
